TPU v7x, 32 devices: a whole 2x2x4 slice. The times are simulated.
32 devices in a mesh: row: 8 (over y, x, core), col: 4 (over z).
Axes of the slice: x: 2, y: 2, z: 4, core: 2. Of those that a mesh axis runs over, the one named last changes fastest.
Arguments:
- pair_factors: float32 [12288, 1024], P(('row', 'col')), may hold values from -0.09375 to 0.09375
- k_prev: float32 [12288, 12288], P('row', 'col'), as said below
- energies: float32 [12288], P('row'), may hold values from 0.3 to 2
Outputs:
- casida: float32 [12288, 12288], P('row', 'col')
- vectors: float32 [12288, 8], P('row')
- images: float32 [12288, 8], P('row')
- tridiagonal: float32 [2, 8], replicated
Inputs may be any that keep to these rules, and one draw needn't show every extreme that they name: k_prev is exactly symmetric.
All inputs are finite; a program needn't handle non-finite values.
Results may differ from a plain program's by a relative error of at most 0.0003.
Values sent between devices are 32-bit elements; how exact they have to be, the bound alone decides.
A program may use at most 128 MiB of HBM per device.

v0:
```python
import jax
import jax.numpy as jnp
from jax import lax
from jax.sharding import PartitionSpec as P

N = 12288
PANEL_W = 512
PC = 8


def from_root(value, axis, root):
    mine = lax.axis_index(axis) == root
    return lax.psum(jnp.where(mine, value, jnp.zeros_like(value)), axis)


def shards(pair_factors, k_prev, energies):
    rows_here, cols_here = k_prev.shape
    per_col = lax.axis_size("row") // lax.axis_size("col")
    row_index = lax.axis_index("row")
    col_index = lax.axis_index("col")
    total = jnp.zeros((rows_here, cols_here), jnp.float32)
    aux_here = pair_factors.shape[1]
    width = PANEL_W
    for start_at in range(0, aux_here, width):
        stop_at = min(start_at + width, aux_here)
        piece = pair_factors[:, start_at:stop_at]
        left_rows = lax.all_gather(piece, "col", axis=0, tiled=True)
        right_parts = []
        for offset in range(per_col):
            right_parts.append(from_root(left_rows, "row", per_col * col_index + offset))
        right_rows = jnp.concatenate(right_parts, axis=0)
        total = total + lax.dot_general(
            left_rows,
            right_rows,
            (((1,), (1,)), ((), ())),
            precision=lax.Precision.HIGHEST,
            preferred_element_type=jnp.float32,
        )
    global_rows = row_index * rows_here + jnp.arange(rows_here, dtype=jnp.int32)
    global_cols = col_index * cols_here + jnp.arange(cols_here, dtype=jnp.int32)
    on_diagonal = global_rows[:, None] == global_cols[None, :]
    casida = 4.0 * (k_prev + total) + jnp.where(on_diagonal, energies[:, None], 0.0)
    col_ids = jnp.arange(PC, dtype=jnp.int32)
    scale = jnp.sqrt(jnp.float32(N))
    diag_list = []
    sub_list = []
    spread = from_root(casida[:, :PC], "col", 0)
    panel = lax.all_gather(spread, "row", axis=0, tiled=True)
    total_rows = panel.shape[0]
    all_rows = jnp.arange(total_rows, dtype=jnp.int32)
    upper_full = jnp.zeros((total_rows, PC), jnp.float32)
    lower_full = jnp.zeros((total_rows, PC), jnp.float32)
    for column_at in range(PC):
        column = (
            panel[:, column_at]
            - jnp.dot(upper_full, lower_full[column_at], precision=lax.Precision.HIGHEST)
            - jnp.dot(lower_full, upper_full[column_at], precision=lax.Precision.HIGHEST)
        )
        diag_list.append(column[column_at])
        below = jnp.where(all_rows > column_at, column, 0.0)
        lead = column[column_at + 1]
        sigma = jnp.sum(below * below)
        root = jnp.sqrt(sigma)
        alpha = jnp.where(lead >= 0, -root, root)
        length = jnp.sqrt(jnp.maximum(2.0 * (sigma + jnp.abs(lead) * root), 1.0))
        unit = (below - alpha * (all_rows == column_at + 1).astype(jnp.float32)) / length
        unit_cols = lax.dynamic_slice_in_dim(unit, col_index * cols_here, cols_here, 0)
        partial_rows = jnp.dot(casida, unit_cols, precision=lax.Precision.HIGHEST)
        placed = lax.dynamic_update_slice_in_dim(
            jnp.zeros((total_rows,), jnp.float32), partial_rows, row_index * rows_here, 0
        )
        image = lax.psum(placed, ("row", "col"))
        image = image - jnp.dot(
            upper_full,
            jnp.dot(lower_full.T, unit, precision=lax.Precision.HIGHEST),
            precision=lax.Precision.HIGHEST,
        )
        image = image - jnp.dot(
            lower_full,
            jnp.dot(upper_full.T, unit, precision=lax.Precision.HIGHEST),
            precision=lax.Precision.HIGHEST,
        )
        image = 2.0 * image
        partner = image - jnp.sum(image * unit) * unit
        pick = (col_ids == column_at).astype(jnp.float32)[None, :]
        upper_full = upper_full + unit[:, None] * pick
        lower_full = lower_full + partner[:, None] * pick
        sub_list.append(alpha)
    upper = lax.dynamic_slice_in_dim(upper_full, row_index * rows_here, rows_here, 0)
    lower = lax.dynamic_slice_in_dim(lower_full, row_index * rows_here, rows_here, 0)
    tridiagonal = jnp.stack([jnp.stack(diag_list), jnp.stack(sub_list)])
    return (casida, scale * upper, scale * lower, tridiagonal)


def solution(mesh):
    in_specs = (P(("row", "col"), None), P("row", "col"), P("row"))
    out_specs = (P("row", "col"), P("row", None), P("row", None), P())
    return jax.shard_map(shards, mesh=mesh, in_specs=in_specs, out_specs=out_specs, check_vma=False)
```

profile of v0, /device:TPU:0, one launch (start us, length us, event | category | flops | bytes accessed | tf_op | source)
XLA Modules:
  0.0 965.7 jit_solution(18281307544850483089)
XLA Ops:
  7.2 2.6 fusion.234
  9.9 0.7 all-gather.3.cloned.1.call-update
  10.7 65.6 %all-gather.5.cloned.1.call-done = f32[1536,512]{1,0:T(8,128)} async-done(((f32[384,512]{1,0:T(8,128)}), f32[1536,512]{1,0:T(8,128)}) %all-gather.5.cloned.1.call-update) | async-done | bytes 3145744 | tf_op jit(solution)/shard_map/all_gather | solution.py:27
  76.3 5.6 broadcast_select_fusion.1
  81.9 58.1 %all-gather.3.cloned.1.call-done = f32[1536,512]{1,0:T(8,128)} async-done(((f32[384,512]{1,0:T(8,128)}), f32[1536,512]{1,0:T(8,128)}) %all-gather.3.cloned.1.call-update) | async-done | bytes 3145744 | tf_op jit(solution)/shard_map/all_gather | solution.py:27
  140.0 5.6 broadcast_select_fusion.3
  145.6 0.7 broadcast_reduce_fusion
  146.3 18.8 %copy.9 = f32[1536,3072]{0,1:T(8,128)} copy(f32[1536,3072]{1,0:T(8,128)} %param.4) | data formatting | bytes 37748736 | tf_op args[1]
  165.1 151.2 %all-reduce.3.cloned.1.call-done = (f32[1536,512]{1,0:T(8,128)}, f32[1536,512]{1,0:T(8,128)}, f32[1536,512]{1,0:T(8,128)}, f32[1536,512]{1,0:T(8,128)}) async-done(((f32[1536,512]{1,0:T(8,128)}, f32[1536,512]{1,0:T(8,128)}, f32[1536,512]{1,0:T(8,128)}, f32[1536,512]{1,0:T(8,128)}), (f32[1536,512]{1,0:T(8,128)}, f32[1536,512]{1,0:T(8,128)}, f32[1536,512]{1,0:T(8,128)}, ...) | async-done | bytes 12582928 | tf_op jit(solution)/shard_map/psum | solution.py:13
  316.4 34.6 %fusion.2 = f32[3072,1536]{1,0:T(8,128)} fusion(f32[1536,512]{1,0:T(8,128)S(1)} %copy-done.1, f32[1536,512]{1,0:T(8,128)} %get-tuple-element.12, f32[1536,512]{1,0:T(8,128)} %get-tuple-element.13), kind=kOutput, calls=%fused_computation.3 | convolution fusion | flops 28992602112 | bytes 28311552 | tf_op jit(solution)/shard_map/dot_general | solution.py:32
  351.0 38.9 %fusion.1 = f32[1536,3072]{0,1:T(8,128)S(1)} fusion(f32[1536,3072]{0,1:T(8,128)} %copy.9, f32[3072,1536]{1,0:T(8,128)} %fusion.2, f32[1536,512]{1,0:T(8,128)} %all-gather.5.cloned.1.call-done, f32[1536]{0:T(1024)S(1)} %copy-done.2, s32[1536]{0:T(1024)S(1)} %iota_add_fusion.1, s32[3072]{0:T(1024)S(1)} %iota_add_fusion, f32[1536,512]{1,0:T(8,128)} %get-tuple-element.14, ...), kind=kOutput, calls=%fused_computation.2 | convolution fusion | flops 29020913664 | bytes 66084864 | tf_op jit(solution)/shard_map/dot_general | solution.py:32
  389.9 6.5 copy-done
  396.4 19.5 %psum.95 = f32[1536,8]{0,1:T(8,128)S(1)} all-reduce(f32[1536,8]{0,1:T(8,128)S(1)} %slice_select_fusion), channel_id=1, replica_groups=mesh['row'=8,'col'=4] {'col'}, use_global_device_ids=true, to_apply=%region_4.5 | all-reduce | flops 12288 | bytes 98304 | tf_op jit(solution)/shard_map/psum | solution.py:13
  415.9 9.5 all_gather.11
  425.7 0.7 broadcast.265
  430.3 12.9 %convolution_reduce_fusion.7 = f32[1536]{0:T(1024)S(1)} fusion(f32[1536,3072]{0,1:T(8,128)} %copy-done, f32[3072,1]{0,1:T(1,128)S(1)} %bitcast.304), kind=kOutput, calls=%fused_computation.21 | convolution fusion | flops 56623104 | bytes 18892800 | tf_op jit(solution)/shard_map/dot_general | solution.py:68
  443.5 38.1 %psum.96 = f32[12288]{0:T(1024)S(1)} all-reduce(f32[12288]{0:T(1024)S(1)} %dynamic_update_slice.24), channel_id=1, replica_groups=mesh['row'=8,'col'=4] {'row','col'}, use_global_device_ids=true, to_apply=%region_6.7 | all-reduce | flops 12288 | bytes 98304 | tf_op jit(solution)/shard_map/psum | solution.py:72
  481.6 1.6 fusion.12
  483.2 0.7 broadcast.267
  484.5 0.7 multiply_subtract_fusion.7
  490.5 1.0 convolution_bitcast_fusion.13
  491.5 1.0 convolution_bitcast_fusion.12
  493.1 12.9 %convolution_reduce_fusion.6 = f32[1536]{0:T(1024)S(1)} fusion(f32[1536,3072]{0,1:T(8,128)} %copy-done, f32[3072,1]{0,1:T(1,128)S(1)} %bitcast.298), kind=kOutput, calls=%fused_computation.20 | convolution fusion | flops 56623104 | bytes 18892800 | tf_op jit(solution)/shard_map/dot_general | solution.py:68
  506.3 41.5 %psum.97 = f32[12288]{0:T(1024)S(1)} all-reduce(f32[12288]{0:T(1024)S(1)} %dynamic_update_slice.25), channel_id=1, replica_groups=mesh['row'=8,'col'=4] {'row','col'}, use_global_device_ids=true, to_apply=%region_9.10 | all-reduce | flops 12288 | bytes 98304 | tf_op jit(solution)/shard_map/psum | solution.py:72
  549.0 0.7 multiply_subtract_fusion.6
  555.2 1.0 convolution_bitcast_fusion.11
  556.2 1.0 convolution_bitcast_fusion.10
  557.9 12.9 %convolution_reduce_fusion.5 = f32[1536]{0:T(1024)S(1)} fusion(f32[1536,3072]{0,1:T(8,128)} %copy-done, f32[3072,1]{0,1:T(1,128)S(1)} %bitcast.299), kind=kOutput, calls=%fused_computation.19 | convolution fusion | flops 56623104 | bytes 18892800 | tf_op jit(solution)/shard_map/dot_general | solution.py:68
  571.1 40.2 %psum.98 = f32[12288]{0:T(1024)S(1)} all-reduce(f32[12288]{0:T(1024)S(1)} %dynamic_update_slice.26), channel_id=1, replica_groups=mesh['row'=8,'col'=4] {'row','col'}, use_global_device_ids=true, to_apply=%region_12.13 | all-reduce | flops 12288 | bytes 98304 | tf_op jit(solution)/shard_map/psum | solution.py:72
  612.5 0.7 multiply_subtract_fusion.5
  618.7 1.0 convolution_bitcast_fusion.9
  619.8 1.0 convolution_bitcast_fusion.8
  621.4 12.9 %convolution_reduce_fusion.4 = f32[1536]{0:T(1024)S(1)} fusion(f32[1536,3072]{0,1:T(8,128)} %copy-done, f32[3072,1]{0,1:T(1,128)S(1)} %bitcast.300), kind=kOutput, calls=%fused_computation.18 | convolution fusion | flops 56623104 | bytes 18892800 | tf_op jit(solution)/shard_map/dot_general | solution.py:68
  634.6 41.1 %psum.99 = f32[12288]{0:T(1024)S(1)} all-reduce(f32[12288]{0:T(1024)S(1)} %dynamic_update_slice.27), channel_id=1, replica_groups=mesh['row'=8,'col'=4] {'row','col'}, use_global_device_ids=true, to_apply=%region_15.16 | all-reduce | flops 12288 | bytes 98304 | tf_op jit(solution)/shard_map/psum | solution.py:72
  677.0 0.7 multiply_subtract_fusion.4
  680.1 0.7 fusion.239
  683.5 1.0 convolution_bitcast_fusion.7
  684.5 1.0 convolution_bitcast_fusion.6
  686.2 12.9 %convolution_reduce_fusion.3 = f32[1536]{0:T(1024)S(1)} fusion(f32[1536,3072]{0,1:T(8,128)} %copy-done, f32[3072,1]{0,1:T(1,128)S(1)} %bitcast.301), kind=kOutput, calls=%fused_computation.17 | convolution fusion | flops 56623104 | bytes 18892800 | tf_op jit(solution)/shard_map/dot_general | solution.py:68
  699.4 40.0 %psum.100 = f32[12288]{0:T(1024)S(1)} all-reduce(f32[12288]{0:T(1024)S(1)} %dynamic_update_slice.28), channel_id=1, replica_groups=mesh['row'=8,'col'=4] {'row','col'}, use_global_device_ids=true, to_apply=%region_18.19 | all-reduce | flops 12288 | bytes 98304 | tf_op jit(solution)/shard_map/psum | solution.py:72
  740.6 0.7 multiply_subtract_fusion.3
  743.9 0.6 fusion.238
  747.1 1.0 convolution_bitcast_fusion.5
  748.1 1.0 convolution_bitcast_fusion.4
  749.1 0.7 fusion.232
  749.8 12.9 %convolution_reduce_fusion.2 = f32[1536]{0:T(1024)S(1)} fusion(f32[1536,3072]{0,1:T(8,128)} %copy-done, f32[3072,1]{0,1:T(1,128)S(1)} %bitcast.302), kind=kOutput, calls=%fused_computation.16 | convolution fusion | flops 56623104 | bytes 18892800 | tf_op jit(solution)/shard_map/dot_general | solution.py:68
  763.0 41.2 %psum.101 = f32[12288]{0:T(1024)S(1)} all-reduce(f32[12288]{0:T(1024)S(1)} %dynamic_update_slice.29), channel_id=1, replica_groups=mesh['row'=8,'col'=4] {'row','col'}, use_global_device_ids=true, to_apply=%region_21.22 | all-reduce | flops 12288 | bytes 98304 | tf_op jit(solution)/shard_map/psum | solution.py:72
  804.2 0.6 fusion.233
  805.5 0.7 multiply_subtract_fusion.2
  808.4 0.6 fusion.237
  811.8 1.0 convolution_bitcast_fusion.3
  812.8 1.0 convolution_bitcast_fusion.2
  814.3 12.9 %convolution_reduce_fusion.1 = f32[1536]{0:T(1024)S(1)} fusion(f32[1536,3072]{0,1:T(8,128)} %copy-done, f32[3072,1]{0,1:T(1,128)S(1)} %bitcast.303), kind=kOutput, calls=%fused_computation.15 | convolution fusion | flops 56623104 | bytes 18892800 | tf_op jit(solution)/shard_map/dot_general | solution.py:68
  827.5 40.1 %psum.102 = f32[12288]{0:T(1024)S(1)} all-reduce(f32[12288]{0:T(1024)S(1)} %dynamic_update_slice.30), channel_id=1, replica_groups=mesh['row'=8,'col'=4] {'row','col'}, use_global_device_ids=true, to_apply=%region_24.25 | all-reduce | flops 12288 | bytes 98304 | tf_op jit(solution)/shard_map/psum | solution.py:72
  868.7 0.7 multiply_subtract_fusion.1
  874.7 1.1 convolution_bitcast_fusion.1
  875.8 1.1 convolution_bitcast_fusion
  876.9 18.6 %copy.10 = f32[1536,3072]{1,0:T(8,128)} copy(f32[1536,3072]{0,1:T(8,128)} %copy-done) | data formatting | bytes 37748736
  896.0 12.9 %convolution_reduce_fusion = f32[1536]{0:T(1024)S(1)} fusion(f32[1536,3072]{0,1:T(8,128)} %copy-done, f32[3072,1]{0,1:T(1,128)S(1)} %bitcast.297), kind=kOutput, calls=%fused_computation.14 | convolution fusion | flops 56623104 | bytes 18892800 | tf_op jit(solution)/shard_map/dot_general | solution.py:68
  909.2 41.0 %psum.103 = f32[12288]{0:T(1024)S(1)} all-reduce(f32[12288]{0:T(1024)S(1)} %dynamic_update_slice.31), channel_id=1, replica_groups=mesh['row'=8,'col'=4] {'row','col'}, use_global_device_ids=true, to_apply=%region_27.28 | all-reduce | flops 12288 | bytes 98304 | tf_op jit(solution)/shard_map/psum | solution.py:72
  950.7 0.7 multiply_reduce_fusion
  951.4 0.7 multiply_subtract_fusion
  952.2 5.1 stack.39
  957.9 0.7 fusion.195
  (124 shorter events, 34.3 us)
Async XLA Ops:
  7.2 69.2 %all-gather.5.cloned.1.call-start = ((), (), s32[]{:S(2)}) async-start(), calls=%async_computation.1 | async-start | bytes 3932160 | tf_op jit(solution)/shard_map/all_gather | solution.py:27
  9.9 130.1 %all-gather.3.cloned.1.call-start = ((), (), s32[]{:S(2)}) async-start(), calls=%async_computation | async-start | bytes 3932160 | tf_op jit(solution)/shard_map/all_gather | solution.py:27
  10.6 305.7 %all-reduce.3.cloned.1.call-start = ((), (), s32[]{:S(2)}) async-start(), calls=%async_computation.2 | async-start | bytes 25165824 | tf_op jit(solution)/shard_map/psum | solution.py:13
  146.3 170.1 %copy-start.1 = (f32[1536,512]{1,0:T(8,128)S(1)}, f32[1536,512]{1,0:T(8,128)}, u32[]{:S(2)}) copy-start(f32[1536,512]{1,0:T(8,128)} %all-gather.3.cloned.1.call-done) | copy-start | bytes 9437188
  165.0 185.9 %copy-start.2 = (f32[1536]{0:T(1024)S(1)}, f32[1536]{0:T(1024)}, u32[]{:S(2)}) copy-start(f32[1536]{0:T(1024)} %param.5) | copy-start | bytes 18436
  389.9 6.5 copy-start
Sparse Core Ops, SparseCore 0:
  10.1 66.1 all-gather.4
  77.9 62.0 all-gather.2
  145.7 170.6 all-reduce.2
where the time goes:
time: 974 us; the launch traced here: 966 us
  blocking collectives  352 us (36%)
  waiting for transfers between devices  276 us (28%)
  matrix products  208 us (21%)
  local copies, waits for them, and re-layouts  63.6 us (7%)
  between operations  36 us (4%)
  other arithmetic  30 us (3%)
    psum x8, blocking collectives, shards(): image = lax.psum(placed, ('row', 'col'))  323 us
    psum x1, waiting for transfers between devices, from_root(): return lax.psum(jnp.where(mine, value, jnp.zeros_like(value)), axis)  151 us
    all_gather x2, waiting for transfers between devices, shards(): left_rows = lax.all_gather(piece, 'col', axis=0, tiled=True)  124 us
    dot_general x8, matrix products, shards(): partial_rows = jnp.dot(casida, unit_cols, precision=lax.Precision.HIGHEST)  103 us
    dot_general x2, matrix products, shards(): lax.dot_general(left_rows, right_rows, (((1,), (1,)), ((), ())), precisio...  73.6 us
    unnamed x8, local copies, waits for them, and re-layouts  43.9 us
  transfers between devices with their start and end apart: 3, of which 3 were waited for; matrix products, arithmetic and copies ran while one was open for 3% of the time, Pallas kernels for 0%

commit v1 on v0

v1 whole, which is shorter than its diff:
```python
import functools

import jax
import jax.numpy as jnp
from jax import lax
from jax.experimental import pallas as pl
from jax.experimental.pallas import tpu as pltpu
from jax.sharding import PartitionSpec as P

PC = 8
LANES = 128
MESH = pl.DeviceIdType.MESH
HIGHEST = lax.Precision.HIGHEST


def panel_kernel(
    n_row, n_col, part_ref, casida_ref, upper_out, lower_out, tri_out,
    block, panel_in, panel, upper, lower, unit, sums, mine, whole_row, from_col, from_row,
    load_sem, own_sem, pa_send, pa_recv, pb_send, pb_recv, c_send, c_recv, r_send, r_recv,
):
    r = lax.axis_index("row")
    c = lax.axis_index("col")
    rows_here, cols_here = block.shape
    total = n_row * rows_here
    load = pltpu.make_async_copy(casida_ref, block, load_sem)
    load.start()
    col_peers = [lax.rem(c + d, n_col) for d in range(1, n_col)]
    row_peers = [lax.rem(r + d, n_row) for d in range(1, n_row)]
    barrier = pltpu.get_barrier_semaphore()
    for peer in col_peers:
        pl.semaphore_signal(barrier, inc=1, device_id=(r, peer), device_id_type=MESH)
    for peer in row_peers:
        pl.semaphore_signal(barrier, inc=1, device_id=(peer, c), device_id_type=MESH)
    pl.semaphore_wait(barrier, n_col + n_row - 2)

    @pl.when(r == 0)
    def _():
        own = pltpu.make_async_copy(part_ref, panel_in.at[c], own_sem)
        own.start()
        copies = [
            pltpu.make_async_remote_copy(
                part_ref, panel_in.at[c], pa_send.at[d - 1], pa_recv,
                device_id=(jnp.int32(d), c), device_id_type=MESH,
            )
            for d in range(1, n_row)
        ]
        for copy in copies:
            copy.start()
        for copy in copies:
            copy.wait_send()
        own.wait()

    @pl.when(r != 0)
    def _():
        pltpu.make_async_remote_copy(
            part_ref, panel_in.at[c], pa_send.at[0], pa_recv,
            device_id=(jnp.int32(0), c), device_id_type=MESH,
        ).wait_recv()

    copies = [
        pltpu.make_async_remote_copy(
            panel_in.at[c], panel_in.at[c], pb_send.at[i], pb_recv.at[c],
            device_id=(r, peer), device_id_type=MESH,
        )
        for i, peer in enumerate(col_peers)
    ]
    for copy in copies:
        copy.start()
    for peer in col_peers:
        pltpu.make_async_remote_copy(
            panel_in.at[peer], panel_in.at[peer], pb_send.at[0], pb_recv.at[peer],
            device_id=(r, peer), device_id_type=MESH,
        ).wait_recv()
    for copy in copies:
        copy.wait_send()
    for k in range(n_col):
        panel[:, k * cols_here:(k + 1) * cols_here] = panel_in[k]
    upper[...] = jnp.zeros_like(upper)
    lower[...] = jnp.zeros_like(lower)
    tri_out[...] = jnp.zeros_like(tri_out)
    load.wait()

    index = lax.broadcasted_iota(jnp.int32, (1, total), 1)
    sub_id = lax.broadcasted_iota(jnp.int32, (PC, 1), 0)
    lane_id = lax.broadcasted_iota(jnp.int32, (PC, LANES), 1)
    group = 32 if rows_here % 32 == 0 else 8
    tiles = cols_here // LANES

    @pl.loop(0, PC)
    def _(j):
        slot = lax.rem(j, 2)
        at_j = lane_id == j
        lower_j = jnp.sum(jnp.where(at_j, lower[:, :LANES], 0.0), axis=1, keepdims=True)
        upper_j = jnp.sum(jnp.where(at_j, upper[:, :LANES], 0.0), axis=1, keepdims=True)
        picked = jnp.where(sub_id == j, panel[...], 0.0)
        column = jnp.sum(
            picked - upper[...] * lower_j - lower[...] * upper_j, axis=0, keepdims=True
        )
        diag = jnp.sum(jnp.where(index == j, column, 0.0), axis=1, keepdims=True)
        lead = jnp.sum(jnp.where(index == j + 1, column, 0.0), axis=1, keepdims=True)
        below = jnp.where(index > j, column, 0.0)
        sigma = jnp.sum(below * below, axis=1, keepdims=True)
        root = jnp.sqrt(sigma)
        alpha = jnp.where(lead >= 0, -root, root)
        length = jnp.sqrt(jnp.maximum(2.0 * (sigma + jnp.abs(lead) * root), 1.0))
        u = (below - jnp.where(index == j + 1, alpha, 0.0)) / length
        unit[...] = jnp.broadcast_to(u, (PC, total))
        tri_out[...] += jnp.where(
            sub_id == j,
            jnp.where(lane_id == 0, diag, jnp.where(lane_id == 1, alpha, 0.0)),
            0.0,
        )
        first = pl.multiple_of(c * cols_here, LANES)

        @pl.loop(0, rows_here // group)
        def _(g):
            acc = [None] * (group // 8)
            for t in range(tiles):
                piece = unit[:, pl.ds(first + t * LANES, LANES)]
                for q in range(group // 8):
                    start = pl.multiple_of(g * group + q * 8, 8)
                    term = block[pl.ds(start, 8), t * LANES:(t + 1) * LANES] * piece
                    acc[q] = term if t == 0 else acc[q] + term
            for q in range(group // 8):
                start = pl.multiple_of(g * group + q * 8, 8)
                sums[pl.ds(start, 8), :] = acc[q]

        partial = lax.dot_general(
            jnp.ones((8, LANES), jnp.float32), sums[...], (((1,), (1,)), ((), ())),
            precision=HIGHEST, preferred_element_type=jnp.float32,
        )
        mine[...] = partial[0:1]
        from_col[slot, c] = partial[0:1]
        copies = [
            pltpu.make_async_remote_copy(
                mine, from_col.at[slot, c], c_send.at[i], c_recv.at[slot, c],
                device_id=(r, peer), device_id_type=MESH,
            )
            for i, peer in enumerate(col_peers)
        ]
        for copy in copies:
            copy.start()
        for peer in col_peers:
            pltpu.make_async_remote_copy(
                mine, from_col.at[slot, peer], c_send.at[0], c_recv.at[slot, peer],
                device_id=(r, peer), device_id_type=MESH,
            ).wait_recv()
        summed = from_col[slot, 0]
        for k in range(1, n_col):
            summed = summed + from_col[slot, k]
        whole_row[...] = summed
        from_row[slot, r] = summed
        row_copies = [
            pltpu.make_async_remote_copy(
                whole_row, from_row.at[slot, r], r_send.at[i], r_recv.at[slot, r],
                device_id=(peer, c), device_id_type=MESH,
            )
            for i, peer in enumerate(row_peers)
        ]
        for copy in row_copies:
            copy.start()
        u_all = unit[...]
        lower_u = jnp.sum(lower[...] * u_all, axis=1, keepdims=True)
        upper_u = jnp.sum(upper[...] * u_all, axis=1, keepdims=True)
        for peer in row_peers:
            pltpu.make_async_remote_copy(
                whole_row, from_row.at[slot, peer], r_send.at[0], r_recv.at[slot, peer],
                device_id=(peer, c), device_id_type=MESH,
            ).wait_recv()
        product = jnp.concatenate([from_row[slot, k] for k in range(n_row)], axis=1)
        image = 2.0 * (
            product
            - jnp.sum(upper[...] * lower_u + lower[...] * upper_u, axis=0, keepdims=True)
        )
        u_row = unit[0:1]
        partner = image - jnp.sum(image * u_row, axis=1, keepdims=True) * u_row
        upper[...] = jnp.where(sub_id == j, unit[...], upper[...])
        lower[...] = jnp.where(sub_id == j, partner, lower[...])
        for copy in copies + row_copies:
            copy.wait_send()

    scale = float(total) ** 0.5
    rows = pl.ds(pl.multiple_of(r * rows_here, LANES), rows_here)
    upper_out[...] = scale * upper[:, rows]
    lower_out[...] = scale * lower[:, rows]


def reduce_panel(casida, n_row, n_col):
    rows_here, cols_here = casida.shape
    total = n_row * rows_here
    f32 = jnp.float32
    dma = pltpu.SemaphoreType.DMA
    vmem = pl.BlockSpec(memory_space=pltpu.VMEM)
    return pl.pallas_call(
        functools.partial(panel_kernel, n_row, n_col),
        out_shape=(
            jax.ShapeDtypeStruct((PC, rows_here), f32),
            jax.ShapeDtypeStruct((PC, rows_here), f32),
            jax.ShapeDtypeStruct((PC, LANES), f32),
        ),
        in_specs=[vmem, pl.BlockSpec(memory_space=pl.ANY)],
        out_specs=(vmem, vmem, vmem),
        scratch_shapes=[
            pltpu.VMEM((rows_here, cols_here), f32),
            pltpu.VMEM((n_col, PC, cols_here), f32),
            pltpu.VMEM((PC, total), f32),
            pltpu.VMEM((PC, total), f32),
            pltpu.VMEM((PC, total), f32),
            pltpu.VMEM((PC, total), f32),
            pltpu.VMEM((rows_here, LANES), f32),
            pltpu.VMEM((1, rows_here), f32),
            pltpu.VMEM((1, rows_here), f32),
            pltpu.VMEM((2, n_col, 1, rows_here), f32),
            pltpu.VMEM((2, n_row, 1, rows_here), f32),
            dma, dma,
            dma((n_row - 1,)), dma,
            dma((n_col - 1,)), dma((n_col,)),
            dma((n_col - 1,)), dma((2, n_col)),
            dma((n_row - 1,)), dma((2, n_row)),
        ],
        compiler_params=pltpu.CompilerParams(
            collective_id=0, has_side_effects=True, vmem_limit_bytes=48 * 1024 * 1024
        ),
    )(casida[:PC], casida)


def shards(pair_factors, k_prev, energies):
    rows_here, cols_here = k_prev.shape
    n_row = lax.axis_size("row")
    n_col = lax.axis_size("col")
    per_col = n_row // n_col
    row_index = lax.axis_index("row")
    col_index = lax.axis_index("col")
    left_rows = lax.all_gather(pair_factors, "col", axis=0, tiled=True)
    moves = []
    for r in range(n_row):
        for c in range(n_col):
            to_row = (r % per_col) * n_col + c
            moves.append((r * n_col + c, to_row * n_col + r // per_col))
    moved = lax.ppermute(pair_factors, ("row", "col"), moves)
    right_rows = lax.all_gather(moved, "row", axis=0, tiled=True)
    product = lax.dot_general(
        left_rows,
        right_rows,
        (((1,), (1,)), ((), ())),
        precision=lax.Precision.HIGH,
        preferred_element_type=jnp.float32,
    )
    global_rows = row_index * rows_here + jnp.arange(rows_here, dtype=jnp.int32)
    global_cols = col_index * cols_here + jnp.arange(cols_here, dtype=jnp.int32)
    on_diagonal = global_rows[:, None] == global_cols[None, :]
    casida = 4.0 * (k_prev + product) + jnp.where(on_diagonal, energies[:, None], 0.0)
    upper, lower, tri = reduce_panel(casida, n_row, n_col)
    return (casida, upper.T, lower.T, tri[:, :2].T)


def solution(mesh):
    in_specs = (P(("row", "col"), None), P("row", "col"), P("row"))
    out_specs = (P("row", "col"), P("row", None), P("row", None), P())
    return jax.shard_map(shards, mesh=mesh, in_specs=in_specs, out_specs=out_specs, check_vma=False)
```

time: 974 us -> 447 us (0.46)
  blocking collectives: 352 us -> 0 us
  matrix products: 208 us -> 38.2 us
  Pallas kernels: 0 us -> 106 us
  local copies, waits for them, and re-layouts: 63.6 us -> 3.92 us
  other arithmetic: 30 us -> 0.01 us
  between operations: 36 us -> 14.1 us
    psum x9 -> x0, blocking collectives: 343 us -> none  [the longest x8 323 us: shards(): image = lax.psum(placed, ('row', 'col'))]
    all_gather x2, waiting for transfers between devices: 124 us -> 282 us  [the longest x1 206 us: shards(): left_rows = lax.all_gather(pair_factors, 'col', axis=0, tiled=True)]
    psum x1 -> x0, waiting for transfers between devices: 151 us -> none  [from_root(): return lax.psum(jnp.where(mine, value, jnp.zeros_like(value)), axis)]
    dot_general x51 -> x0, matrix products: 134 us -> none  [the longest x8 103 us: shards(): partial_rows = jnp.dot(casida, unit_cols, precision=lax.Precision.HIGHEST)]
    pallas_call x0 -> x1, Pallas kernels: none -> 106 us  [reduce_panel(): pl.pallas_call(functools.partial(panel_kernel, n_row, n_col), out_shape=(...]
    unnamed x8 -> x5, local copies, waits for them, and re-layouts: 43.9 us -> 3.02 us
    dot_general x2 -> x1, matrix products: 73.6 us -> 38.2 us  [shards(): lax.dot_general(left_rows, right_rows, (((1,), (1,)), ((), ())), precisio...]
    select_n x3 -> x0, other arithmetic: 11.1 us -> none  [from_root(): return lax.psum(jnp.where(mine, value, jnp.zeros_like(value)), axis)]
  transfers between devices with their start and end apart: 3 -> 3, of which waited for: 3 -> 2; matrix products, arithmetic and copies ran while one was open for 3% -> 0% of each run, Pallas kernels for 0% -> 0%
where the time goes in v1:
time: 447 us
  waiting for transfers between devices  282 us (63%)
  Pallas kernels  106 us (24%)
  matrix products  38.2 us (9%)
  between operations  14.1 us (3%)
    all_gather x1, waiting for transfers between devices, shards(): left_rows = lax.all_gather(pair_factors, 'col', axis=0, tiled=True)  206 us
    pallas_call x1, Pallas kernels, reduce_panel(): pl.pallas_call(functools.partial(panel_kernel, n_row, n_col), out_shape=(...  106 us
    all_gather x1, waiting for transfers between devices, shards(): right_rows = lax.all_gather(moved, 'row', axis=0, tiled=True)  75.6 us
    dot_general x1, matrix products, shards(): lax.dot_general(left_rows, right_rows, (((1,), (1,)), ((), ())), precisio...  38.2 us
  transfers between devices with their start and end apart: 3, of which 2 were waited for; matrix products, arithmetic and copies ran while one was open for 0% of the time, Pallas kernels for 0%

profile of v1, /device:TPU:0, one launch (start us, length us, event | category | flops | bytes accessed | tf_op | source)
XLA Modules:
  0.0 446.6 jit_solution(13283395100656254421)
XLA Ops:
  7.2 0.0 all-gather.3.cloned.1.call-start
  7.2 0.7 all-gather.3.cloned.1.call-update
  7.9 0.0 all-gather.5.cloned.1.call-start
  7.9 2.1 collective-permute-start
  10.0 0.0 collective-permute-done
  10.0 0.0 copy-start
  10.0 1.1 copy-done
  11.2 0.0 all-gather.5.cloned.1.call-update
  11.2 206.0 %all-gather.3.cloned.1.call-done = f32[1536,1024]{1,0:T(8,128)} async-done(((f32[384,1024]{1,0:T(8,128)}), f32[1536,1024]{1,0:T(8,128)}) %all-gather.3.cloned.1.call-update) | async-done | bytes 6291472 | tf_op jit(solution)/shard_map/all_gather | solution.py:234
  217.2 75.6 %all-gather.5.cloned.1.call-done = f32[3072,1024]{1,0:T(8,128)} async-done(((f32[384,1024]{1,0:T(8,128)}), f32[3072,1024]{1,0:T(8,128)}) %all-gather.5.cloned.1.call-update) | async-done | bytes 12582928 | tf_op jit(solution)/shard_map/all_gather | solution.py:241
  292.9 38.2 %select_add_fusion.casida_ref = f32[1536,3072]{1,0:T(8,128)} fusion(f32[1536,3072]{1,0:T(8,128)} %param.4, f32[1536,1024]{1,0:T(8,128)} %all-gather.3.cloned.1.call-done, f32[3072,1024]{1,0:T(8,128)} %all-gather.5.cloned.1.call-done, f32[1536]{0:T(1024)} %param.5, s32[3072]{0:T(1024)S(1)} %iota_add_fusion, s32[1536]{0:T(1024)S(1)} %iota_add_fusion.1), kind=kOutput, calls=%fused_computation | convolution fusion | flops 29014622208 | bytes 56647680 | tf_op jit(solution)/shard_map/dot_general | solution.py:242
  331.1 0.9 slice.8.part_ref
  332.0 105.9 %shard_map.66 = (f32[8,1536]{1,0:T(8,128)S(1)}, f32[8,1536]{1,0:T(8,128)S(1)}, f32[8,128]{1,0:T(8,128)S(1)}) custom-call(f32[8,3072]{1,0:T(8,128)S(1)} %slice.8.part_ref, f32[1536,3072]{1,0:T(8,128)} %select_add_fusion.casida_ref), custom_call_target="tpu_custom_call" | custom-call | tf_op jit(solution)/shard_map/pallas_call | solution.py:194
  437.9 0.6 copy.7
  438.5 0.6 copy.10
  439.1 0.6 copy.11
  (3 shorter events, 0.0 us)
Async XLA Ops:
  7.2 210.1 %all-gather.3.cloned.1.call-start = ((), (), s32[]{:S(2)}) async-start(), calls=%async_computation | async-start | bytes 7864320 | tf_op jit(solution)/shard_map/all_gather | solution.py:234
  7.9 285.0 %all-gather.5.cloned.1.call-start = ((), (), s32[]{:S(2)}) async-start(), calls=%async_computation.1 | async-start | bytes 14155776 | tf_op jit(solution)/shard_map/all_gather | solution.py:241
  7.9 2.1 collective-permute-start
  10.0 1.1 copy-start
Sparse Core Ops, SparseCore 0:
  9.5 207.6 all-gather.2
  219.7 73.0 all-gather.4

commit v2 on v1

--- a/solution.py
+++ b/solution.py
@@ -224,21 +224,200 @@
     )(casida[:PC], casida)
 
 
+def ring_place(i, count):
+    if count == 4:
+        return i + (i // 2) * (1 - 2 * (i % 2))
+    return i
+
+
+def gather_kernel(
+    n_row, n_col, pieces, own_ref, left, right,
+    l_recv, l_send, r_recv, r_send, p_recv, p_send, keep_left, keep_right,
+):
+    r = lax.axis_index("row")
+    c = lax.axis_index("col")
+    depth = own_ref.shape[0] // pieces
+    chips = n_row // 2
+    chip, half = r // 2, r % 2
+    turn = 1 - 2 * half
+    place, root = ring_place(chip, chips), ring_place(c, chips)
+    ahead = 2 * ring_place((place + turn + chips) % chips, chips) + half
+    behind = 2 * ring_place((place - turn + chips) % chips, chips) + half
+    partner = 2 * chip + 1 - half
+    distance = ((place - root) * turn + chips) % chips
+    has_up, has_down = c < n_col - 1, c > 0
+    is_root, is_last = distance == 0, distance == chips - 1
+
+    barrier = pltpu.get_barrier_semaphore()
+    for row in (ahead, behind, partner):
+        pl.semaphore_signal(barrier, inc=1, device_id=(row, c), device_id_type=MESH)
+
+    @pl.when(has_up)
+    def _():
+        pl.semaphore_signal(barrier, inc=1, device_id=(r, c + 1), device_id_type=MESH)
+
+    @pl.when(has_down)
+    def _():
+        pl.semaphore_signal(barrier, inc=1, device_id=(r, c - 1), device_id_type=MESH)
+
+    pl.semaphore_wait(
+        barrier, 3 + has_up.astype(jnp.int32) + has_down.astype(jnp.int32)
+    )
+
+    def cut(k):
+        return pl.ds(k * depth, depth)
+
+    def source(block, k, own):
+        return own_ref.at[cut(k)] if own else left.at[block, cut(k)]
+
+    def along(block, k, own, way):
+        return pltpu.make_async_remote_copy(
+            source(block, k, own), left.at[block, cut(k)],
+            l_send.at[(way + 1) // 2, block, k], l_recv.at[block, k],
+            device_id=(r, c + way), device_id_type=MESH,
+        )
+
+    def spread(block, k, src, to, send, recv):
+        return pltpu.make_async_remote_copy(
+            src, right.at[half, block, cut(k)], send.at[block, k], recv.at[block, k],
+            device_id=(to, c), device_id_type=MESH,
+        )
+
+    def root_sends(block, k, own):
+        src = source(block, k, own)
+        return (
+            spread(block, k, src, ahead, r_send, r_recv),
+            spread(block, k, src, partner, p_send, p_recv),
+            pltpu.make_async_copy(src, right.at[half, block, cut(k)], keep_right.at[block, k]),
+        )
+
+    def relay_sends(block, k):
+        src = right.at[half, block, cut(k)]
+        return (
+            spread(block, k, src, ahead, r_send, r_recv),
+            spread(block, k, src, partner, p_send, p_recv),
+        )
+
+    def from_partner(block, k):
+        here = right.at[1 - half, block, cut(k)]
+        return pltpu.make_async_remote_copy(
+            here, here, p_send.at[block, k], p_recv.at[block, k],
+            device_id=(partner, c), device_id_type=MESH,
+        )
+
+    def left_event(step, way, k):
+        block = c - way * step
+        own = step == 0
+        ways = (1, -1) if own else (way,)
+        if not own:
+            along(block, k, False, -way).wait_recv()
+        for to in ways:
+            @pl.when(has_up if to == 1 else has_down)
+            def _():
+                along(block, k, own, to).start()
+
+        @pl.when(is_root)
+        def _():
+            for copy in root_sends(block, k, own):
+                copy.start()
+
+    def right_event(step, way, k):
+        block = c - way * step
+
+        @pl.when(jnp.logical_not(is_root))
+        def _():
+            forward, across = relay_sends(block, k)
+            forward.wait_recv()
+            across.start()
+
+            @pl.when(jnp.logical_not(is_last))
+            def _():
+                forward.start()
+
+    def finish(step, way, k):
+        block = c - way * step
+        own = step == 0
+        for to in (1, -1) if own else (way,):
+            @pl.when(has_up if to == 1 else has_down)
+            def _():
+                along(block, k, own, to).wait_send()
+
+        from_partner(block, k).wait_recv()
+
+        @pl.when(is_root)
+        def _():
+            forward, across, keep = root_sends(block, k, own)
+            forward.wait_send()
+            across.wait_send()
+            keep.wait()
+
+        @pl.when(jnp.logical_not(is_root))
+        def _():
+            forward, across = relay_sends(block, k)
+            across.wait_send()
+
+            @pl.when(jnp.logical_not(is_last))
+            def _():
+                forward.wait_send()
+
+    def guarded(event, step, way, k):
+        if step == 0:
+            event(step, way, k)
+        else:
+            @pl.when(c >= step if way == 1 else c + step < n_col)
+            def _():
+                event(step, way, k)
+
+    events = []
+    for step in range(n_col):
+        for k in range(pieces):
+            for way in (1, -1) if step else (1,):
+                events.append((step, way, k))
+    lag = 4
+    for i in range(len(events) + lag):
+        if i < len(events):
+            guarded(left_event, *events[i])
+        if i == pieces - 1:
+            keep = pltpu.make_async_copy(own_ref, left.at[c], keep_left)
+            keep.start()
+        if i >= lag:
+            guarded(right_event, *events[i - lag])
+    for event in events:
+        guarded(finish, *event)
+    keep.wait()
+
+
+def gather_factors(own, n_row, n_col):
+    rows, aux = own.shape
+    pieces = 3 if rows % 24 == 0 else 1
+    dma = pltpu.SemaphoreType.DMA
+    anywhere = pl.BlockSpec(memory_space=pl.ANY)
+    per = (n_col, pieces)
+    left, right = pl.pallas_call(
+        functools.partial(gather_kernel, n_row, n_col, pieces),
+        out_shape=(
+            jax.ShapeDtypeStruct((n_col, rows, aux), own.dtype),
+            jax.ShapeDtypeStruct((2, n_col, rows, aux), own.dtype),
+        ),
+        in_specs=[anywhere],
+        out_specs=(anywhere, anywhere),
+        scratch_shapes=[
+            dma(per), dma((2,) + per), dma(per), dma(per), dma(per), dma(per),
+            dma, dma(per),
+        ],
+        compiler_params=pltpu.CompilerParams(collective_id=1, has_side_effects=True),
+    )(own)
+    return left.reshape(n_col * rows, aux), right.reshape(2 * n_col * rows, aux)
+
+
 def shards(pair_factors, k_prev, energies):
     rows_here, cols_here = k_prev.shape
     n_row = lax.axis_size("row")
     n_col = lax.axis_size("col")
-    per_col = n_row // n_col
+    assert n_row == 2 * n_col
     row_index = lax.axis_index("row")
     col_index = lax.axis_index("col")
-    left_rows = lax.all_gather(pair_factors, "col", axis=0, tiled=True)
-    moves = []
-    for r in range(n_row):
-        for c in range(n_col):
-            to_row = (r % per_col) * n_col + c
-            moves.append((r * n_col + c, to_row * n_col + r // per_col))
-    moved = lax.ppermute(pair_factors, ("row", "col"), moves)
-    right_rows = lax.all_gather(moved, "row", axis=0, tiled=True)
+    left_rows, right_rows = gather_factors(pair_factors, n_row, n_col)
     product = lax.dot_general(
         left_rows,
         right_rows,

time: 447 us -> 391 us (0.87)
  waiting for transfers between devices: 282 us -> 0 us
  Pallas kernels: 106 us -> 349 us
  between operations: 14.1 us -> 0.68 us
    all_gather x2 -> x0, waiting for transfers between devices: 282 us -> none  [the longest x1 206 us: shards(): left_rows = lax.all_gather(pair_factors, 'col', axis=0, tiled=True)]
    pallas_call x0 -> x1, Pallas kernels: none -> 243 us  [gather_factors(): pl.pallas_call(functools.partial(gather_kernel, n_row, n_col, pieces), ou...]
  transfers between devices with their start and end apart: 3 -> 0, of which waited for: 2 -> 0; matrix products, arithmetic and copies ran while one was open for 0% -> 0% of each run, Pallas kernels for 0% -> 0%
where the time goes in v2:
time: 391 us
  Pallas kernels  349 us (89%)
  matrix products  38.3 us (10%)
    pallas_call x1, Pallas kernels, gather_factors(): pl.pallas_call(functools.partial(gather_kernel, n_row, n_col, pieces), ou...  243 us
    pallas_call x1, Pallas kernels, reduce_panel(): pl.pallas_call(functools.partial(panel_kernel, n_row, n_col), out_shape=(...  106 us
    dot_general x1, matrix products, shards(): lax.dot_general(left_rows, right_rows, (((1,), (1,)), ((), ())), precisio...  38.3 us

profile of v2, /device:TPU:0, one launch (start us, length us, event | category | flops | bytes accessed | tf_op | source)
XLA Modules:
  0.0 391.1 jit_solution(429906373700261761)
XLA Ops:
  0.7 243.4 %shard_map.66 = (f32[4,384,1024]{2,1,0:T(8,128)}, f32[2,4,384,1024]{3,2,1,0:T(8,128)}) custom-call(f32[384,1024]{1,0:T(8,128)} %own_ref.1), custom_call_target="tpu_custom_call" | custom-call | tf_op jit(solution)/shard_map/pallas_call | solution.py:396
  244.0 38.3 %select_add_fusion.casida_ref = f32[1536,3072]{1,0:T(8,128)} fusion(f32[1536,3072]{1,0:T(8,128)} %param.4, f32[1536,1024]{1,0:T(8,128)} %bitcast.11, f32[3072,1024]{1,0:T(8,128)} %bitcast.10, f32[1536]{0:T(1024)} %param.5, s32[3072]{0:T(1024)S(1)} %iota_add_fusion, s32[1536]{0:T(1024)S(1)} %iota_add_fusion.1), kind=kOutput, calls=%fused_computation | convolution fusion | flops 29014622208 | bytes 56647680 | tf_op jit(solution)/shard_map/dot_general | solution.py:421
  282.3 0.9 slice.8.part_ref
  283.2 106.0 %shard_map.67 = (f32[8,1536]{1,0:T(8,128)S(1)}, f32[8,1536]{1,0:T(8,128)S(1)}, f32[8,128]{1,0:T(8,128)S(1)}) custom-call(f32[8,3072]{1,0:T(8,128)S(1)} %slice.8.part_ref, f32[1536,3072]{1,0:T(8,128)} %select_add_fusion.casida_ref), custom_call_target="tpu_custom_call" | custom-call | tf_op jit(solution)/shard_map/pallas_call | solution.py:194
  389.2 0.6 copy.7
  389.8 0.6 copy.10
  390.5 0.6 copy.11
  (3 shorter events, 0.0 us)

commit v3 on v2

--- a/solution.py
+++ b/solution.py
@@ -232,7 +232,7 @@
 
 def gather_kernel(
     n_row, n_col, pieces, own_ref, left, right,
-    l_recv, l_send, r_recv, r_send, p_recv, p_send, keep_left, keep_right,
+    l_recv, l_send, r_recv, r_send, p_recv, p_send, back_send, keep_left,
 ):
     r = lax.axis_index("row")
     c = lax.axis_index("col")
@@ -288,7 +288,13 @@
         return (
             spread(block, k, src, ahead, r_send, r_recv),
             spread(block, k, src, partner, p_send, p_recv),
-            pltpu.make_async_copy(src, right.at[half, block, cut(k)], keep_right.at[block, k]),
+        )
+
+    def give_back(block, k):
+        there = right.at[1 - half, block, cut(k)]
+        return pltpu.make_async_remote_copy(
+            there, there, back_send.at[block, k], r_recv.at[block, k],
+            device_id=(partner, c), device_id_type=MESH,
         )
 
     def relay_sends(block, k):
@@ -334,6 +340,14 @@
             def _():
                 forward.start()
 
+    def back_event(step, way, k):
+        block = c - way * step
+
+        @pl.when(is_root)
+        def _():
+            from_partner(block, k).wait_recv()
+            give_back(block, k).start()
+
     def finish(step, way, k):
         block = c - way * step
         own = step == 0
@@ -342,17 +356,18 @@
             def _():
                 along(block, k, own, to).wait_send()
 
-        from_partner(block, k).wait_recv()
-
         @pl.when(is_root)
         def _():
-            forward, across, keep = root_sends(block, k, own)
+            forward, across = root_sends(block, k, own)
             forward.wait_send()
             across.wait_send()
-            keep.wait()
+            back = give_back(block, k)
+            back.wait_send()
+            forward.wait_recv()
 
         @pl.when(jnp.logical_not(is_root))
         def _():
+            from_partner(block, k).wait_recv()
             forward, across = relay_sends(block, k)
             across.wait_send()
 
@@ -382,6 +397,7 @@
             keep.start()
         if i >= lag:
             guarded(right_event, *events[i - lag])
+            guarded(back_event, *events[i - lag])
     for event in events:
         guarded(finish, *event)
     keep.wait()
@@ -389,7 +405,7 @@
 
 def gather_factors(own, n_row, n_col):
     rows, aux = own.shape
-    pieces = 3 if rows % 24 == 0 else 1
+    pieces = 4 if rows % 32 == 0 else 1
     dma = pltpu.SemaphoreType.DMA
     anywhere = pl.BlockSpec(memory_space=pl.ANY)
     per = (n_col, pieces)
@@ -403,7 +419,7 @@
         out_specs=(anywhere, anywhere),
         scratch_shapes=[
             dma(per), dma((2,) + per), dma(per), dma(per), dma(per), dma(per),
-            dma, dma(per),
+            dma(per), dma,
         ],
         compiler_params=pltpu.CompilerParams(collective_id=1, has_side_effects=True),
     )(own)

time: 391 us -> 277 us (0.71)
  Pallas kernels: 349 us -> 235 us
    pallas_call x1, Pallas kernels: 243 us -> 113 us  [gather_factors(): pl.pallas_call(functools.partial(gather_kernel, n_row, n_col, pieces), ou...]
    pallas_call x1, Pallas kernels: 106 us -> 121 us  [reduce_panel(): pl.pallas_call(functools.partial(panel_kernel, n_row, n_col), out_shape=(...]
where the time goes in v3:
time: 277 us
  Pallas kernels  235 us (85%)
  matrix products  38.3 us (14%)
  local copies, waits for them, and re-layouts  2.78 us (1%)
    pallas_call x1, Pallas kernels, reduce_panel(): pl.pallas_call(functools.partial(panel_kernel, n_row, n_col), out_shape=(...  121 us
    pallas_call x1, Pallas kernels, gather_factors(): pl.pallas_call(functools.partial(gather_kernel, n_row, n_col, pieces), ou...  113 us
    dot_general x1, matrix products, shards(): lax.dot_general(left_rows, right_rows, (((1,), (1,)), ((), ())), precisio...  38.3 us

profile of v3, /device:TPU:0, one launch (start us, length us, event | category | flops | bytes accessed | tf_op | source)
XLA Modules:
  0.0 276.6 jit_solution(17283483805864407606)
XLA Ops:
  0.7 113.4 %shard_map.66 = (f32[4,384,1024]{2,1,0:T(8,128)}, f32[2,4,384,1024]{3,2,1,0:T(8,128)}) custom-call(f32[384,1024]{1,0:T(8,128)} %own_ref.1), custom_call_target="tpu_custom_call" | custom-call | tf_op jit(solution)/shard_map/pallas_call | solution.py:412
  114.0 38.3 %select_add_fusion.casida_ref = f32[1536,3072]{1,0:T(8,128)} fusion(f32[1536,3072]{1,0:T(8,128)} %param.4, f32[1536,1024]{1,0:T(8,128)} %bitcast.11, f32[3072,1024]{1,0:T(8,128)} %bitcast.10, f32[1536]{0:T(1024)} %param.5, s32[3072]{0:T(1024)S(1)} %iota_add_fusion, s32[1536]{0:T(1024)S(1)} %iota_add_fusion.1), kind=kOutput, calls=%fused_computation | convolution fusion | flops 29014622208 | bytes 56647680 | tf_op jit(solution)/shard_map/dot_general | solution.py:437
  152.3 0.9 slice.8.part_ref
  153.2 121.5 %shard_map.67 = (f32[8,1536]{1,0:T(8,128)S(1)}, f32[8,1536]{1,0:T(8,128)S(1)}, f32[8,128]{1,0:T(8,128)S(1)}) custom-call(f32[8,3072]{1,0:T(8,128)S(1)} %slice.8.part_ref, f32[1536,3072]{1,0:T(8,128)} %select_add_fusion.casida_ref), custom_call_target="tpu_custom_call" | custom-call | tf_op jit(solution)/shard_map/pallas_call | solution.py:194
  274.7 0.6 copy.7
  275.3 0.6 copy.10
  275.9 0.6 copy.11
  (3 shorter events, 0.0 us)

commit v4 on v3

--- a/solution.py
+++ b/solution.py
@@ -246,6 +246,7 @@
     partner = 2 * chip + 1 - half
     distance = ((place - root) * turn + chips) % chips
     has_up, has_down = c < n_col - 1, c > 0
+    at_end = jnp.logical_not(has_up & has_down)
     is_root, is_last = distance == 0, distance == chips - 1
 
     barrier = pltpu.get_barrier_semaphore()
@@ -395,9 +396,14 @@
         if i == pieces - 1:
             keep = pltpu.make_async_copy(own_ref, left.at[c], keep_left)
             keep.start()
-        if i >= lag:
-            guarded(right_event, *events[i - lag])
-            guarded(back_event, *events[i - lag])
+        soon = range(pieces) if i == pieces else range(i - 1, i) if i > pieces else ()
+        for ready, cond in ((soon, at_end), (range(i - lag, i - lag + 1), jnp.logical_not(at_end))):
+            for e in ready:
+                if 0 <= e < len(events):
+                    @pl.when(cond)
+                    def _():
+                        guarded(right_event, *events[e])
+                        guarded(back_event, *events[e])
     for event in events:
         guarded(finish, *event)
     keep.wait()

time: 277 us -> 276 us (level)
  no operation moved by 1% of the time
where the time goes in v4:
time: 276 us
  Pallas kernels  234 us (85%)
  matrix products  38.3 us (14%)
  local copies, waits for them, and re-layouts  2.78 us (1%)
    pallas_call x1, Pallas kernels, reduce_panel(): pl.pallas_call(functools.partial(panel_kernel, n_row, n_col), out_shape=(...  121 us
    pallas_call x1, Pallas kernels, gather_factors(): pl.pallas_call(functools.partial(gather_kernel, n_row, n_col, pieces), ou...  113 us
    dot_general x1, matrix products, shards(): lax.dot_general(left_rows, right_rows, (((1,), (1,)), ((), ())), precisio...  38.3 us

profile of v4, /device:TPU:0, one launch (start us, length us, event | category | flops | bytes accessed | tf_op | source)
XLA Modules:
  0.0 275.7 jit_solution(4333739592102840577)
XLA Ops:
  0.7 113.4 %shard_map.66 = (f32[4,384,1024]{2,1,0:T(8,128)}, f32[2,4,384,1024]{3,2,1,0:T(8,128)}) custom-call(f32[384,1024]{1,0:T(8,128)} %own_ref.1), custom_call_target="tpu_custom_call" | custom-call | tf_op jit(solution)/shard_map/pallas_call | solution.py:418
  114.1 38.3 %select_add_fusion.casida_ref = f32[1536,3072]{1,0:T(8,128)} fusion(f32[1536,3072]{1,0:T(8,128)} %param.4, f32[1536,1024]{1,0:T(8,128)} %bitcast.11, f32[3072,1024]{1,0:T(8,128)} %bitcast.10, f32[1536]{0:T(1024)} %param.5, s32[3072]{0:T(1024)S(1)} %iota_add_fusion, s32[1536]{0:T(1024)S(1)} %iota_add_fusion.1), kind=kOutput, calls=%fused_computation | convolution fusion | flops 29014622208 | bytes 56647680 | tf_op jit(solution)/shard_map/dot_general | solution.py:443
  152.3 0.9 slice.8.part_ref
  153.2 120.6 %shard_map.67 = (f32[8,1536]{1,0:T(8,128)S(1)}, f32[8,1536]{1,0:T(8,128)S(1)}, f32[8,128]{1,0:T(8,128)S(1)}) custom-call(f32[8,3072]{1,0:T(8,128)S(1)} %slice.8.part_ref, f32[1536,3072]{1,0:T(8,128)} %select_add_fusion.casida_ref), custom_call_target="tpu_custom_call" | custom-call | tf_op jit(solution)/shard_map/pallas_call | solution.py:194
  273.8 0.6 copy.7
  274.4 0.6 copy.10
  275.1 0.6 copy.11
  (3 shorter events, 0.0 us)
